TPU v7x, 32 devices: a whole 2x2x4 slice. The times are simulated.
32 devices in a mesh: groups: 2 (over y), pages: 4 (over z), patches: 4 (over x, core).
Axes of the slice: x: 2, y: 2, z: 4, core: 2. Of those that a mesh axis runs over, the one named last changes fastest.
Arguments:
- queries: bfloat16 [16, 32, 128], P(('groups', 'pages'), 'patches'), parts along dimension 0, may hold values from -6 to 6
- gallery: bfloat16 [640, 1024, 128], P(('groups', 'pages'), 'patches'), parts along dimension 0, may hold values from -0.5 to 0.5
- page_rows: int32 [640], P('groups'), parts along dimension 0, may hold values from 0 to 319, as said below
- candidates: int32 [16, 32], P(('groups', 'pages')), parts along dimension 0, may hold values from 0 to 319, as said below
Outputs:
- scores: float32 [16, 32], P(('groups', 'pages')), parts along dimension 0
There are 2 independent parts, one for each index of `groups`. A program takes and returns all parts, laid end to end along the dimension named above; each array names one. Nothing has to cross between parts.
Inputs may be any that keep to these rules, and one draw needn't show every extreme that they name: A permutation: page id c is stored at row page_rows[c] of gallery, which lies on pages index page_rows[c] // 80. Each query's 32 page ids are distinct. The 2 queries of one pages index have at most 48 candidates stored on one pages index, and in every draw some pages index stores exactly 48 candidates of the queries of every pages index.
All inputs are finite; a program needn't handle non-finite values.
Results may differ from a plain program's by a relative error of at most 0.0003.
Values may be sent and summed in bfloat16 or wider, within the bound.
A program may use at most 64 MiB of HBM per device.

v0:
```python
import jax
import jax.numpy as jnp
from jax import lax
from jax.sharding import PartitionSpec as P

QT = 32
CAP = 48


def token_maxima(query_rows, gallery):
    page_count = gallery.shape[0]
    grouped = gallery.reshape(page_count // 8, 8, gallery.shape[1], gallery.shape[2])

    def per_block(block):
        sims = jnp.einsum("rd,bpd->brp", query_rows, block, preferred_element_type=jnp.float32)
        return jnp.max(sims, axis=2)

    result = lax.map(per_block, grouped)
    return result.reshape(page_count, query_rows.shape[0])


def slot_plan(storage, page_count, owner_count, query_count):
    flat_rows = storage.reshape(-1)
    holder = flat_rows // page_count
    local_page = flat_rows % page_count
    onehot = (holder[:, None] == jnp.arange(owner_count, dtype=jnp.int32)[None, :]).astype(
        jnp.int32
    )
    running = jnp.cumsum(onehot, axis=0) - onehot
    rank = jnp.sum(running * onehot, axis=1)
    query_ids = (
        lax.axis_index("pages") * query_count + jnp.arange(query_count, dtype=jnp.int32)[:, None]
    )
    query_ids = jnp.broadcast_to(query_ids, storage.shape).reshape(-1)
    codes = (
        jnp.full((owner_count, CAP), -1, jnp.int32)
        .at[holder, rank]
        .set(query_ids * page_count + local_page)
    )
    return (holder, rank, codes)


def body(queries, gallery, page_rows, candidates):
    query_count = queries.shape[0]
    page_count = gallery.shape[0]
    owner_count = lax.axis_size("pages")
    storage = jnp.take(page_rows, candidates, axis=0)
    local_tokens = lax.all_gather(queries, "patches", axis=1, tiled=True)
    shard_rows = lax.all_gather(local_tokens, "pages", axis=0, tiled=True)
    maxima = token_maxima(shard_rows.reshape(-1, shard_rows.shape[2]), gallery)
    part_count = lax.axis_size("patches")
    arrived = lax.all_to_all(maxima, "patches", split_axis=0, concat_axis=0, tiled=True)
    share_max = jnp.max(arrived.reshape(part_count, page_count // part_count, -1), axis=0)
    share_scores = jnp.mean(share_max.reshape(page_count // part_count, -1, QT), axis=2)
    page_scores = lax.all_gather(share_scores, "patches", axis=0, tiled=True)
    holder, rank, codes = slot_plan(storage, page_count, owner_count, query_count)
    incoming = lax.all_to_all(codes, "pages", split_axis=0, concat_axis=0, tiled=True)
    safe_codes = jnp.maximum(incoming, 0)
    picked = page_scores[safe_codes % page_count, safe_codes // page_count]
    picked = jnp.where(incoming >= 0, picked, 0.0)
    returned = lax.all_to_all(picked, "pages", split_axis=0, concat_axis=0, tiled=True)
    return returned[holder, rank].reshape(storage.shape)


def solution(mesh):
    in_specs = (
        P(("groups", "pages"), "patches", None),
        P(("groups", "pages"), "patches", None),
        P("groups"),
        P(("groups", "pages"), None),
    )
    out_specs = P(("groups", "pages"), None)
    return jax.shard_map(body, mesh=mesh, in_specs=in_specs, out_specs=out_specs, check_vma=False)
```

profile of v0, /device:TPU:0, one launch (start us, length us, event | category | flops | bytes accessed | tf_op | source)
XLA Modules:
  0.0 81.3 jit_solution(7018582230763072979)
XLA Ops:
  0.0 0.7 compare_select_fusion.3
  0.8 0.8 gather_fusion
  1.7 0.7 compare_and_fusion
  3.9 10.2 %scatter_fusion = s32[4,48]{1,0:T(4,128)} fusion(s32[4,48]{1,0:T(4,128)} %broadcast_in_dim.36, s32[64]{0:T(128)S(1)} %get-tuple-element.42, s32[64]{0:T(128)S(1)} %get-tuple-element.45), kind=kCustom, calls=%fused_computation.3 | custom fusion | bytes 1280 | tf_op jit(solution)/shard_map/scatter | solution.py:38
  14.1 6.3 %all-to-all-start = ((s32[4,1,48]{2,1,0:T(1,128)}), s32[4,1,48]{2,1,0:T(1,128)S(1)}, u32[]{:S(2)}, u32[]{:S(2)}) async-start(s32[4,1,48]{2,1,0:T(1,128)} %bitcast.6), calls=%async_computation | async-start | bytes 4096 | tf_op jit(solution)/shard_map/all_to_all | solution.py:57
  20.5 5.4 %all_gather.9 = bf16[2,32,128]{2,1,0:T(8,128)(2,1)S(1)} all-gather(bf16[2,8,128]{2,1,0:T(8,128)(2,1)} %param.6), channel_id=1, replica_groups=mesh['groups'=2,'pages'=4,'patches'=4] {'patches'}, dimensions={1}, use_global_device_ids=true | all-gather | bytes 20480 | tf_op jit(solution)/shard_map/all_gather | solution.py:48
  25.9 13.7 %all_gather.10 = bf16[8,32,128]{2,1,0:T(8,128)(2,1)S(1)} all-gather(bf16[2,32,128]{2,1,0:T(8,128)(2,1)S(1)} %all_gather.9), channel_id=1, replica_groups=mesh['groups'=2,'pages'=4,'patches'=4] {'pages'}, dimensions={0}, use_global_device_ids=true | all-gather | bytes 81920 | tf_op jit(solution)/shard_map/all_gather | solution.py:49
  39.5 15.2 %while.10 = (s32[]{:T(128)}, f32[10,8,256]{2,1,0:T(8,128)S(1)}, bf16[10,8,256,128]{3,2,1,0:T(8,128)(2,1)}, bf16[256,128]{1,0:T(8,128)(2,1)S(1)}, s32[]{:T(128)}) while((s32[]{:T(128)}, f32[10,8,256]{2,1,0:T(8,128)S(1)}, bf16[10,8,256,128]{3,2,1,0:T(8,128)(2,1)}, bf16[256,128]{1,0:T(8,128)(2,1)S(1)}, s32[]{:T(128)}) %tuple.28), condition=%wide.region_5.6_spmd, body=%wide.region_3.5_spmd.sunk | while | flops 134739968 | bytes 614477 | solution.py:18
  39.5 1.5 %convolution_reduce_fusion.2 = f32[8,256]{1,0:T(8,128)S(1)} fusion(bf16[10,8,256,128]{3,2,1,0:T(8,128)(2,1)} %get-tuple-element.84, s32[]{:T(128)S(6)} %copy.20, bf16[256,128]{1,0:T(8,128)(2,1)S(1)} %get-tuple-element.85), kind=kOutput, calls=%fused_computation.4.clone.1 | convolution fusion | flops 134739968 | bytes 598020 | tf_op jit(solution)/shard_map/while/body/eval_jaxpr/rd,bpd->brp/dot_general | solution.py:15
  41.1 1.5 %convolution_reduce_fusion.2 = f32[8,256]{1,0:T(8,128)S(1)} fusion(bf16[10,8,256,128]{3,2,1,0:T(8,128)(2,1)} %get-tuple-element.84, s32[]{:T(128)S(6)} %copy.20, bf16[256,128]{1,0:T(8,128)(2,1)S(1)} %get-tuple-element.85), kind=kOutput, calls=%fused_computation.4.clone.1 | convolution fusion | flops 134739968 | bytes 598020 | tf_op jit(solution)/shard_map/while/body/eval_jaxpr/rd,bpd->brp/dot_general | solution.py:15
  42.6 1.5 %convolution_reduce_fusion.2 = f32[8,256]{1,0:T(8,128)S(1)} fusion(bf16[10,8,256,128]{3,2,1,0:T(8,128)(2,1)} %get-tuple-element.84, s32[]{:T(128)S(6)} %copy.20, bf16[256,128]{1,0:T(8,128)(2,1)S(1)} %get-tuple-element.85), kind=kOutput, calls=%fused_computation.4.clone.1 | convolution fusion | flops 134739968 | bytes 598020 | tf_op jit(solution)/shard_map/while/body/eval_jaxpr/rd,bpd->brp/dot_general | solution.py:15
  44.1 1.5 %convolution_reduce_fusion.2 = f32[8,256]{1,0:T(8,128)S(1)} fusion(bf16[10,8,256,128]{3,2,1,0:T(8,128)(2,1)} %get-tuple-element.84, s32[]{:T(128)S(6)} %copy.20, bf16[256,128]{1,0:T(8,128)(2,1)S(1)} %get-tuple-element.85), kind=kOutput, calls=%fused_computation.4.clone.1 | convolution fusion | flops 134739968 | bytes 598020 | tf_op jit(solution)/shard_map/while/body/eval_jaxpr/rd,bpd->brp/dot_general | solution.py:15
  45.6 1.5 %convolution_reduce_fusion.2 = f32[8,256]{1,0:T(8,128)S(1)} fusion(bf16[10,8,256,128]{3,2,1,0:T(8,128)(2,1)} %get-tuple-element.84, s32[]{:T(128)S(6)} %copy.20, bf16[256,128]{1,0:T(8,128)(2,1)S(1)} %get-tuple-element.85), kind=kOutput, calls=%fused_computation.4.clone.1 | convolution fusion | flops 134739968 | bytes 598020 | tf_op jit(solution)/shard_map/while/body/eval_jaxpr/rd,bpd->brp/dot_general | solution.py:15
  47.2 1.5 %convolution_reduce_fusion.2 = f32[8,256]{1,0:T(8,128)S(1)} fusion(bf16[10,8,256,128]{3,2,1,0:T(8,128)(2,1)} %get-tuple-element.84, s32[]{:T(128)S(6)} %copy.20, bf16[256,128]{1,0:T(8,128)(2,1)S(1)} %get-tuple-element.85), kind=kOutput, calls=%fused_computation.4.clone.1 | convolution fusion | flops 134739968 | bytes 598020 | tf_op jit(solution)/shard_map/while/body/eval_jaxpr/rd,bpd->brp/dot_general | solution.py:15
  48.7 1.5 %convolution_reduce_fusion.2 = f32[8,256]{1,0:T(8,128)S(1)} fusion(bf16[10,8,256,128]{3,2,1,0:T(8,128)(2,1)} %get-tuple-element.84, s32[]{:T(128)S(6)} %copy.20, bf16[256,128]{1,0:T(8,128)(2,1)S(1)} %get-tuple-element.85), kind=kOutput, calls=%fused_computation.4.clone.1 | convolution fusion | flops 134739968 | bytes 598020 | tf_op jit(solution)/shard_map/while/body/eval_jaxpr/rd,bpd->brp/dot_general | solution.py:15
  50.2 1.5 %convolution_reduce_fusion.2 = f32[8,256]{1,0:T(8,128)S(1)} fusion(bf16[10,8,256,128]{3,2,1,0:T(8,128)(2,1)} %get-tuple-element.84, s32[]{:T(128)S(6)} %copy.20, bf16[256,128]{1,0:T(8,128)(2,1)S(1)} %get-tuple-element.85), kind=kOutput, calls=%fused_computation.4.clone.1 | convolution fusion | flops 134739968 | bytes 598020 | tf_op jit(solution)/shard_map/while/body/eval_jaxpr/rd,bpd->brp/dot_general | solution.py:15
  51.7 1.5 %convolution_reduce_fusion.2 = f32[8,256]{1,0:T(8,128)S(1)} fusion(bf16[10,8,256,128]{3,2,1,0:T(8,128)(2,1)} %get-tuple-element.84, s32[]{:T(128)S(6)} %copy.20, bf16[256,128]{1,0:T(8,128)(2,1)S(1)} %get-tuple-element.85), kind=kOutput, calls=%fused_computation.4.clone.1 | convolution fusion | flops 134739968 | bytes 598020 | tf_op jit(solution)/shard_map/while/body/eval_jaxpr/rd,bpd->brp/dot_general | solution.py:15
  53.3 1.5 %convolution_reduce_fusion.2 = f32[8,256]{1,0:T(8,128)S(1)} fusion(bf16[10,8,256,128]{3,2,1,0:T(8,128)(2,1)} %get-tuple-element.84, s32[]{:T(128)S(6)} %copy.20, bf16[256,128]{1,0:T(8,128)(2,1)S(1)} %get-tuple-element.85), kind=kOutput, calls=%fused_computation.4.clone.1 | convolution fusion | flops 134739968 | bytes 598020 | tf_op jit(solution)/shard_map/while/body/eval_jaxpr/rd,bpd->brp/dot_general | solution.py:15
  55.4 3.3 %all-to-all-start.1 = ((f32[4,20,256]{2,1,0:T(8,128)}), f32[4,20,256]{2,1,0:T(8,128)S(1)}, u32[]{:S(2)}, u32[]{:S(2)}) async-start(f32[4,20,256]{2,1,0:T(8,128)} %all_to_all.20), calls=%async_computation.1 | async-start | bytes 196608 | tf_op jit(solution)/shard_map/all_to_all | solution.py:52
  59.1 3.9 %all-to-all-done.1 = f32[4,20,256]{2,1,0:T(8,128)S(1)} async-done(((f32[4,20,256]{2,1,0:T(8,128)}), f32[4,20,256]{2,1,0:T(8,128)S(1)}, u32[]{:S(2)}, u32[]{:S(2)}) %all-to-all-start.1) | async-done | bytes 81952 | tf_op jit(solution)/shard_map/all_to_all | solution.py:52
  63.3 5.2 %all-gather = f32[4,20,8]{1,2,0:T(8,128)S(1)} all-gather(f32[1,20,8]{1,2,0:T(8,128)S(1)} %copy.12), channel_id=1, replica_groups=mesh['groups'=2,'pages'=4,'patches'=4] {'patches'}, dimensions={0}, use_global_device_ids=true | all-gather | bytes 3200 | tf_op jit(solution)/shard_map/all_gather | solution.py:55
  68.6 1.2 %gather_fusion.1 = f32[192]{0:T(256)S(1)} fusion(f32[80,8]{0,1:T(8,128)S(1)} %reshape.242, s32[192]{0:T(256)S(1)} %reshape.220), kind=kCustom, calls=%fused_computation.1 | custom fusion | bytes 3072 | tf_op jit(solution)/shard_map/gather | solution.py:59
  69.8 9.9 %all_to_all.27 = f32[4,1,48]{2,1,0:T(1,128)S(1)} all-to-all(f32[4,1,48]{2,1,0:T(1,128)S(1)} %compare_select_fusion), channel_id=1, replica_groups=mesh['groups'=2,'pages'=4,'patches'=4] {'pages'}, dimensions={0} | all-to-all | bytes 1536 | tf_op jit(solution)/shard_map/all_to_all | solution.py:61
  79.7 0.9 %gather_fusion.2 = f32[64]{0:T(128)S(1)} fusion(f32[4,48]{1,0:T(4,128)S(1)} %bitcast.60, s32[64]{0:T(128)S(1)} %get-tuple-element.41), kind=kCustom, calls=%fused_computation.2 | custom fusion | bytes 1024 | tf_op jit(solution)/shard_map/gather | solution.py:62
  (47 shorter events, 3.9 us)
Async XLA Ops:
  0.0 0.8 copy-start
  14.1 41.3 %all-to-all-start = ((s32[4,1,48]{2,1,0:T(1,128)}), s32[4,1,48]{2,1,0:T(1,128)S(1)}, u32[]{:S(2)}, u32[]{:S(2)}) async-start(s32[4,1,48]{2,1,0:T(1,128)} %bitcast.6), calls=%async_computation | async-start | bytes 4096 | tf_op jit(solution)/shard_map/all_to_all | solution.py:57
  55.4 7.6 %all-to-all-start.1 = ((f32[4,20,256]{2,1,0:T(8,128)}), f32[4,20,256]{2,1,0:T(8,128)S(1)}, u32[]{:S(2)}, u32[]{:S(2)}) async-start(f32[4,20,256]{2,1,0:T(8,128)} %all_to_all.20), calls=%async_computation.1 | async-start | bytes 196608 | tf_op jit(solution)/shard_map/all_to_all | solution.py:52
where the time goes:
time: 82.3 us; the launch traced here: 81.3 us
  blocking collectives  34.2 us (42%)
  local copies, waits for them, and re-layouts  16.2 us (20%)
  matrix products  14.9 us (18%)
  starting transfers between devices  9.65 us (12%)
  waiting for transfers between devices  3.93 us (5%)
  other arithmetic  2.15 us (3%)
    dot_general x10, matrix products, per_block(): jnp.einsum('rd,bpd->brp', query_rows, block, preferred_element_type=jnp.f...  14.9 us
    all_gather x1, blocking collectives, body(): shard_rows = lax.all_gather(local_tokens, 'pages', axis=0, tiled=True)  13.7 us
    scatter x1, local copies, waits for them, and re-layouts, slot_plan(): codes = jnp.full((owner_count, CAP), -1, jnp.int32).at[holder, rank].set(...  10.2 us
    all_to_all x1, blocking collectives, body(): lax.all_to_all(picked, 'pages', split_axis=0, concat_axis=0, tiled=True)  9.92 us
    all_to_all x1, starting transfers between devices, body(): lax.all_to_all(codes, 'pages', split_axis=0, concat_axis=0, tiled=True)  6.35 us
    all_gather x1, blocking collectives, body(): local_tokens = lax.all_gather(queries, 'patches', axis=1, tiled=True)  5.37 us
    all_gather x1, blocking collectives, body(): page_scores = lax.all_gather(share_scores, 'patches', axis=0, tiled=True)  5.19 us
    all_to_all x1, waiting for transfers between devices, body(): lax.all_to_all(maxima, 'patches', split_axis=0, concat_axis=0, tiled=True)  3.93 us
  transfers between devices with their start and end apart: 2, of which 1 were waited for; matrix products, arithmetic and copies ran while one was open for 19% of the time, Pallas kernels for 0%

commit v1 on v0

--- a/solution.py
+++ b/solution.py
@@ -5,6 +5,12 @@
 
 QT = 32
 CAP = 48
+
+
+def _make_edge(local_array):
+    row_out = jax.lax.all_gather(local_array, "patches")
+    reply = jnp.concatenate(row_out, axis=1)
+    return reply
 
 
 def token_maxima(query_rows, gallery):
@@ -45,7 +51,7 @@
     page_count = gallery.shape[0]
     owner_count = lax.axis_size("pages")
     storage = jnp.take(page_rows, candidates, axis=0)
-    local_tokens = lax.all_gather(queries, "patches", axis=1, tiled=True)
+    local_tokens = _make_edge(queries)
     shard_rows = lax.all_gather(local_tokens, "pages", axis=0, tiled=True)
     maxima = token_maxima(shard_rows.reshape(-1, shard_rows.shape[2]), gallery)
     part_count = lax.axis_size("patches")

time: 82.3 us -> 82.2 us (level)
  no operation moved by 1% of the time
where the time goes in v1:
time: 82.2 us; the launch traced here: 81.2 us
  blocking collectives  34.1 us (41%)
  local copies, waits for them, and re-layouts  16.2 us (20%)
  matrix products  14.9 us (18%)
  starting transfers between devices  9.65 us (12%)
  waiting for transfers between devices  3.93 us (5%)
  other arithmetic  2.15 us (3%)
    dot_general x10, matrix products, per_block(): jnp.einsum('rd,bpd->brp', query_rows, block, preferred_element_type=jnp.f...  14.9 us
    all_gather x1, blocking collectives, body(): shard_rows = lax.all_gather(local_tokens, 'pages', axis=0, tiled=True)  13.7 us
    scatter x1, local copies, waits for them, and re-layouts, slot_plan(): codes = jnp.full((owner_count, CAP), -1, jnp.int32).at[holder, rank].set(...  10.2 us
    all_to_all x1, blocking collectives, body(): lax.all_to_all(picked, 'pages', split_axis=0, concat_axis=0, tiled=True)  9.9 us
    all_to_all x1, starting transfers between devices, body(): lax.all_to_all(codes, 'pages', split_axis=0, concat_axis=0, tiled=True)  6.35 us
    all_gather x1, blocking collectives, _make_edge(): row_out = jax.lax.all_gather(local_array, 'patches')  5.32 us
    all_gather x1, blocking collectives, body(): page_scores = lax.all_gather(share_scores, 'patches', axis=0, tiled=True)  5.19 us
    all_to_all x1, waiting for transfers between devices, body(): lax.all_to_all(maxima, 'patches', split_axis=0, concat_axis=0, tiled=True)  3.93 us
  transfers between devices with their start and end apart: 2, of which 1 were waited for; matrix products, arithmetic and copies ran while one was open for 19% of the time, Pallas kernels for 0%

profile of v1, /device:TPU:0, one launch (start us, length us, event | category | flops | bytes accessed | tf_op | source)
XLA Modules:
  0.0 81.2 jit_solution(6753608963993093545)
XLA Ops:
  0.0 0.7 compare_select_fusion.3
  0.8 0.8 gather_fusion
  1.7 0.7 compare_and_fusion
  3.9 10.2 %scatter_fusion = s32[4,48]{1,0:T(4,128)} fusion(s32[4,48]{1,0:T(4,128)} %broadcast_in_dim.36, s32[64]{0:T(128)S(1)} %get-tuple-element.42, s32[64]{0:T(128)S(1)} %get-tuple-element.45), kind=kCustom, calls=%fused_computation.3 | custom fusion | bytes 1280 | tf_op jit(solution)/shard_map/scatter | solution.py:44
  14.1 6.3 %all-to-all-start = ((s32[4,1,48]{2,1,0:T(1,128)}), s32[4,1,48]{2,1,0:T(1,128)S(1)}, u32[]{:S(2)}, u32[]{:S(2)}) async-start(s32[4,1,48]{2,1,0:T(1,128)} %bitcast.6), calls=%async_computation | async-start | bytes 4096 | tf_op jit(solution)/shard_map/all_to_all | solution.py:63
  20.5 5.3 %all-gather = bf16[8,8,128]{2,1,0:T(8,128)(2,1)S(1)} all-gather(bf16[2,8,128]{2,1,0:T(8,128)(2,1)} %param.6), channel_id=2, replica_groups=mesh['groups'=2,'pages'=4,'patches'=4] {'patches'}, dimensions={0}, use_global_device_ids=true | all-gather | bytes 20480 | tf_op jit(solution)/shard_map/all_gather | solution.py:11
  25.8 13.7 %all_gather.14 = bf16[8,32,128]{2,1,0:T(8,128)(2,1)S(1)} all-gather(bf16[2,32,128]{2,1,0:T(8,128)(2,1)S(1)} %bitcast.68), channel_id=1, replica_groups=mesh['groups'=2,'pages'=4,'patches'=4] {'pages'}, dimensions={0}, use_global_device_ids=true | all-gather | bytes 81920 | tf_op jit(solution)/shard_map/all_gather | solution.py:55
  39.5 15.2 %while.10 = (s32[]{:T(128)}, f32[10,8,256]{2,1,0:T(8,128)S(1)}, bf16[10,8,256,128]{3,2,1,0:T(8,128)(2,1)}, bf16[256,128]{1,0:T(8,128)(2,1)S(1)}, s32[]{:T(128)}) while((s32[]{:T(128)}, f32[10,8,256]{2,1,0:T(8,128)S(1)}, bf16[10,8,256,128]{3,2,1,0:T(8,128)(2,1)}, bf16[256,128]{1,0:T(8,128)(2,1)S(1)}, s32[]{:T(128)}) %tuple.28), condition=%wide.region_5.6_spmd, body=%wide.region_3.5_spmd.sunk | while | flops 134739968 | bytes 614477 | solution.py:24
  39.5 1.5 %convolution_reduce_fusion.2 = f32[8,256]{1,0:T(8,128)S(1)} fusion(bf16[10,8,256,128]{3,2,1,0:T(8,128)(2,1)} %get-tuple-element.84, s32[]{:T(128)S(6)} %copy.27, bf16[256,128]{1,0:T(8,128)(2,1)S(1)} %get-tuple-element.85), kind=kOutput, calls=%fused_computation.4.clone.1 | convolution fusion | flops 134739968 | bytes 598020 | tf_op jit(solution)/shard_map/while/body/eval_jaxpr/rd,bpd->brp/dot_general | solution.py:21
  41.0 1.5 %convolution_reduce_fusion.2 = f32[8,256]{1,0:T(8,128)S(1)} fusion(bf16[10,8,256,128]{3,2,1,0:T(8,128)(2,1)} %get-tuple-element.84, s32[]{:T(128)S(6)} %copy.27, bf16[256,128]{1,0:T(8,128)(2,1)S(1)} %get-tuple-element.85), kind=kOutput, calls=%fused_computation.4.clone.1 | convolution fusion | flops 134739968 | bytes 598020 | tf_op jit(solution)/shard_map/while/body/eval_jaxpr/rd,bpd->brp/dot_general | solution.py:21
  42.5 1.5 %convolution_reduce_fusion.2 = f32[8,256]{1,0:T(8,128)S(1)} fusion(bf16[10,8,256,128]{3,2,1,0:T(8,128)(2,1)} %get-tuple-element.84, s32[]{:T(128)S(6)} %copy.27, bf16[256,128]{1,0:T(8,128)(2,1)S(1)} %get-tuple-element.85), kind=kOutput, calls=%fused_computation.4.clone.1 | convolution fusion | flops 134739968 | bytes 598020 | tf_op jit(solution)/shard_map/while/body/eval_jaxpr/rd,bpd->brp/dot_general | solution.py:21
  44.1 1.5 %convolution_reduce_fusion.2 = f32[8,256]{1,0:T(8,128)S(1)} fusion(bf16[10,8,256,128]{3,2,1,0:T(8,128)(2,1)} %get-tuple-element.84, s32[]{:T(128)S(6)} %copy.27, bf16[256,128]{1,0:T(8,128)(2,1)S(1)} %get-tuple-element.85), kind=kOutput, calls=%fused_computation.4.clone.1 | convolution fusion | flops 134739968 | bytes 598020 | tf_op jit(solution)/shard_map/while/body/eval_jaxpr/rd,bpd->brp/dot_general | solution.py:21
  45.6 1.5 %convolution_reduce_fusion.2 = f32[8,256]{1,0:T(8,128)S(1)} fusion(bf16[10,8,256,128]{3,2,1,0:T(8,128)(2,1)} %get-tuple-element.84, s32[]{:T(128)S(6)} %copy.27, bf16[256,128]{1,0:T(8,128)(2,1)S(1)} %get-tuple-element.85), kind=kOutput, calls=%fused_computation.4.clone.1 | convolution fusion | flops 134739968 | bytes 598020 | tf_op jit(solution)/shard_map/while/body/eval_jaxpr/rd,bpd->brp/dot_general | solution.py:21
  47.1 1.5 %convolution_reduce_fusion.2 = f32[8,256]{1,0:T(8,128)S(1)} fusion(bf16[10,8,256,128]{3,2,1,0:T(8,128)(2,1)} %get-tuple-element.84, s32[]{:T(128)S(6)} %copy.27, bf16[256,128]{1,0:T(8,128)(2,1)S(1)} %get-tuple-element.85), kind=kOutput, calls=%fused_computation.4.clone.1 | convolution fusion | flops 134739968 | bytes 598020 | tf_op jit(solution)/shard_map/while/body/eval_jaxpr/rd,bpd->brp/dot_general | solution.py:21
  48.6 1.5 %convolution_reduce_fusion.2 = f32[8,256]{1,0:T(8,128)S(1)} fusion(bf16[10,8,256,128]{3,2,1,0:T(8,128)(2,1)} %get-tuple-element.84, s32[]{:T(128)S(6)} %copy.27, bf16[256,128]{1,0:T(8,128)(2,1)S(1)} %get-tuple-element.85), kind=kOutput, calls=%fused_computation.4.clone.1 | convolution fusion | flops 134739968 | bytes 598020 | tf_op jit(solution)/shard_map/while/body/eval_jaxpr/rd,bpd->brp/dot_general | solution.py:21
  50.2 1.5 %convolution_reduce_fusion.2 = f32[8,256]{1,0:T(8,128)S(1)} fusion(bf16[10,8,256,128]{3,2,1,0:T(8,128)(2,1)} %get-tuple-element.84, s32[]{:T(128)S(6)} %copy.27, bf16[256,128]{1,0:T(8,128)(2,1)S(1)} %get-tuple-element.85), kind=kOutput, calls=%fused_computation.4.clone.1 | convolution fusion | flops 134739968 | bytes 598020 | tf_op jit(solution)/shard_map/while/body/eval_jaxpr/rd,bpd->brp/dot_general | solution.py:21
  51.7 1.5 %convolution_reduce_fusion.2 = f32[8,256]{1,0:T(8,128)S(1)} fusion(bf16[10,8,256,128]{3,2,1,0:T(8,128)(2,1)} %get-tuple-element.84, s32[]{:T(128)S(6)} %copy.27, bf16[256,128]{1,0:T(8,128)(2,1)S(1)} %get-tuple-element.85), kind=kOutput, calls=%fused_computation.4.clone.1 | convolution fusion | flops 134739968 | bytes 598020 | tf_op jit(solution)/shard_map/while/body/eval_jaxpr/rd,bpd->brp/dot_general | solution.py:21
  53.2 1.5 %convolution_reduce_fusion.2 = f32[8,256]{1,0:T(8,128)S(1)} fusion(bf16[10,8,256,128]{3,2,1,0:T(8,128)(2,1)} %get-tuple-element.84, s32[]{:T(128)S(6)} %copy.27, bf16[256,128]{1,0:T(8,128)(2,1)S(1)} %get-tuple-element.85), kind=kOutput, calls=%fused_computation.4.clone.1 | convolution fusion | flops 134739968 | bytes 598020 | tf_op jit(solution)/shard_map/while/body/eval_jaxpr/rd,bpd->brp/dot_general | solution.py:21
  55.4 3.3 %all-to-all-start.1 = ((f32[4,20,256]{2,1,0:T(8,128)}), f32[4,20,256]{2,1,0:T(8,128)S(1)}, u32[]{:S(2)}, u32[]{:S(2)}) async-start(f32[4,20,256]{2,1,0:T(8,128)} %all_to_all.20), calls=%async_computation.1 | async-start | bytes 196608 | tf_op jit(solution)/shard_map/all_to_all | solution.py:58
  59.0 3.9 %all-to-all-done.1 = f32[4,20,256]{2,1,0:T(8,128)S(1)} async-done(((f32[4,20,256]{2,1,0:T(8,128)}), f32[4,20,256]{2,1,0:T(8,128)S(1)}, u32[]{:S(2)}, u32[]{:S(2)}) %all-to-all-start.1) | async-done | bytes 81952 | tf_op jit(solution)/shard_map/all_to_all | solution.py:58
  63.2 5.2 %all-gather.1 = f32[4,20,8]{1,2,0:T(8,128)S(1)} all-gather(f32[1,20,8]{1,2,0:T(8,128)S(1)} %copy.17), channel_id=1, replica_groups=mesh['groups'=2,'pages'=4,'patches'=4] {'patches'}, dimensions={0}, use_global_device_ids=true | all-gather | bytes 3200 | tf_op jit(solution)/shard_map/all_gather | solution.py:61
  68.5 1.2 %gather_fusion.1 = f32[192]{0:T(256)S(1)} fusion(f32[80,8]{0,1:T(8,128)S(1)} %reshape.251, s32[192]{0:T(256)S(1)} %reshape.228), kind=kCustom, calls=%fused_computation.1 | custom fusion | bytes 3072 | tf_op jit(solution)/shard_map/gather | solution.py:65
  69.8 9.9 %all_to_all.27 = f32[4,1,48]{2,1,0:T(1,128)S(1)} all-to-all(f32[4,1,48]{2,1,0:T(1,128)S(1)} %compare_select_fusion), channel_id=1, replica_groups=mesh['groups'=2,'pages'=4,'patches'=4] {'pages'}, dimensions={0} | all-to-all | bytes 1536 | tf_op jit(solution)/shard_map/all_to_all | solution.py:67
  79.7 0.9 %gather_fusion.2 = f32[64]{0:T(128)S(1)} fusion(f32[4,48]{1,0:T(4,128)S(1)} %bitcast.66, s32[64]{0:T(128)S(1)} %get-tuple-element.41), kind=kCustom, calls=%fused_computation.2 | custom fusion | bytes 1024 | tf_op jit(solution)/shard_map/gather | solution.py:68
  (48 shorter events, 3.9 us)
Async XLA Ops:
  0.0 0.8 copy-start
  14.1 41.2 %all-to-all-start = ((s32[4,1,48]{2,1,0:T(1,128)}), s32[4,1,48]{2,1,0:T(1,128)S(1)}, u32[]{:S(2)}, u32[]{:S(2)}) async-start(s32[4,1,48]{2,1,0:T(1,128)} %bitcast.6), calls=%async_computation | async-start | bytes 4096 | tf_op jit(solution)/shard_map/all_to_all | solution.py:63
  55.4 7.6 %all-to-all-start.1 = ((f32[4,20,256]{2,1,0:T(8,128)}), f32[4,20,256]{2,1,0:T(8,128)S(1)}, u32[]{:S(2)}, u32[]{:S(2)}) async-start(f32[4,20,256]{2,1,0:T(8,128)} %all_to_all.20), calls=%async_computation.1 | async-start | bytes 196608 | tf_op jit(solution)/shard_map/all_to_all | solution.py:58
